TPU v7x, 32 devices: a whole 2x2x4 slice. The times are simulated.
32 devices in a mesh: rep: 2 (over core), tab: 16 (over z, y, x).
Axes of the slice: x: 2, y: 2, z: 4, core: 2. Of those that a mesh axis runs over, the one named last changes fastest.
Arguments:
- grad_out: bfloat16 [8192, 16, 128], P(('rep', 'tab')), may hold values from -1.5 to 1.5
- indices: int32 [16, 8192], P('tab', 'rep'), may hold values from 0 to 1023
- projections: bfloat16 [16, 128, 128], P('tab'), may hold values from -0.75 to 0.75
- widths: int32 [16], replicated, may hold values from 16 to 128
- hot_ids: int32 [16, 32], P('tab'), may hold values from 0 to 1023, as said below
Outputs:
- cold_grad: float32 [2, 16, 1024, 128], P('rep', 'tab')
- hot_grad: float32 [16, 32, 128], P('tab', 'rep')
Inputs may be any that keep to these rules, and one draw needn't show every extreme that they name: `hot_ids`: the 32 hot rows of one table are distinct.
All inputs are finite; a program needn't handle non-finite values.
Results may differ from a plain program's by a relative error of at most 0.005.
Values may be sent and summed in bfloat16 or wider, within the bound.
No kernel may reach another device: no remote copies, remote signals or barrier semaphores. Data moves between devices by JAX's collectives and lax.ppermute only.
A program may use at most 128 MiB of HBM per device.

v0:
```python
import math
import jax
import jax.numpy as jnp
from jax import lax
from jax.sharding import PartitionSpec as P

ROWS = 1024


def swapped(block, axis, bit):
    count = lax.axis_size(axis)
    route = []
    for low in range(count):
        high = low | 1 << bit
        if high != low and high < count:
            route += [(low, high), (high, low)]
    return lax.ppermute(block, axis, route)


def block_sums(narrow_rows, lookups):
    total_len = narrow_rows.shape[0]
    block_len = math.gcd(total_len, 4096)
    turn_count = total_len // block_len
    positions = lax.broadcasted_iota(jnp.int32, (1, ROWS), 1)

    def add_block(block, totals):
        piece_rows = lax.dynamic_slice_in_dim(narrow_rows, block * block_len, block_len, 0)
        row_ids = lax.dynamic_slice_in_dim(lookups, block * block_len, block_len, 0)
        onehot = (row_ids[:, None] == positions).astype(jnp.bfloat16)
        return totals + lax.dot_general(
            onehot, piece_rows, (((0,), (0,)), ((), ())), preferred_element_type=jnp.float32
        )

    start_sums = jnp.zeros((ROWS, narrow_rows.shape[1]), jnp.float32)
    return lax.fori_loop(0, turn_count, add_block, start_sums)


def shards(grad_out, indices, projections, widths, hot_ids):
    tab_dev = projections.shape[0]
    base_width = projections.shape[2]
    columns = lax.broadcasted_iota(jnp.int32, (1, 1, base_width), 2)
    first_table = lax.axis_index("tab") * tab_dev
    own_widths = lax.dynamic_slice_in_dim(widths, first_table, tab_dev, 0)
    received = lax.all_to_all(grad_out, "tab", split_axis=1, concat_axis=0, tiled=True)
    full_proj = jnp.einsum(
        "bte,tej->tbj", received, projections, preferred_element_type=jnp.float32
    )
    narrow = jnp.where(columns < own_widths[:, None, None], full_proj, 0.0).astype(jnp.bfloat16)
    table_grads = [block_sums(narrow[0], indices[0])]
    row_grads = jnp.stack(table_grads)
    own_hot = jnp.take_along_axis(row_grads, hot_ids[:, :, None], axis=1)
    half_hot = hot_ids.shape[1] // 2
    replica = lax.axis_index("rep")
    kept_rows = lax.dynamic_slice_in_dim(own_hot, replica * half_hot, half_hot, 1)
    given_rows = lax.dynamic_slice_in_dim(own_hot, (1 - replica) * half_hot, half_hot, 1)
    partner = swapped(given_rows, "rep", 0)
    hot_grad = kept_rows + partner
    all_rows = lax.broadcasted_iota(jnp.int32, (1, 1, ROWS), 2)
    is_hot = jnp.any(hot_ids[:, :, None] == all_rows, axis=1)
    cold_grad = jnp.where(is_hot[:, :, None], jnp.float32(0.0), row_grads)
    return (cold_grad[None], hot_grad)


def solution(mesh):
    placed = (
        P(("rep", "tab"), None, None),
        P("tab", "rep"),
        P("tab", None, None),
        P(),
        P("tab", None),
    )
    return jax.shard_map(
        shards,
        mesh=mesh,
        in_specs=placed,
        out_specs=(P("rep", "tab", None, None), P("tab", "rep", None)),
        check_vma=False,
    )
```

profile of v0, /device:TPU:9, one launch (start us, length us, event | category | flops | bytes accessed | tf_op | source)
XLA Modules:
  0.0 44.1 jit_solution(15511810765626345854)
XLA Ops:
  0.6 0.0 copy-start
  0.6 2.5 %copy.8 = bf16[256,16,128]{2,0,1:T(8,128)(2,1)} copy(bf16[256,16,128]{2,1,0:T(8,128)(2,1)} %param.5) | data formatting | bytes 2097152 | tf_op args[0]
  3.1 0.0 copy-start.2
  3.1 0.0 copy-start.3
  3.1 0.0 copy-start.1
  3.1 6.8 %all-to-all-start = ((bf16[256,16,128]{2,0,1:T(8,128)(2,1)}), bf16[256,16,128]{2,0,1:T(8,128)(2,1)S(1)}, u32[]{:S(2)}, u32[]{:S(2)}) async-start(bf16[256,16,128]{2,0,1:T(8,128)(2,1)} %copy.8), calls=%async_computation | async-start | bytes 2097152 | tf_op jit(solution)/shard_map/all_to_all | solution.py:44
  9.9 0.0 copy-done.2
  9.9 0.6 %dynamic_slice.13 = s32[1]{0:T(128)} dynamic-slice(s32[16]{0:T(128)S(1)} %copy-done.2, s32[]{:T(128)S(6)} %select_n.55), dynamic_slice_sizes={1} | dynamic-slice | bytes 12 | tf_op jit(solution)/shard_map/dynamic_slice | solution.py:43
  10.5 0.6 %iota_compare_fusion.3 = pred[128]{0:T(512)(128)(4,1)S(1)} fusion(s32[]{:T(128)} %bitcast.2), kind=kLoop, calls=%fused_computation.20 | loop fusion | flops 128 | bytes 132 | tf_op jit(solution)/shard_map/lt | solution.py:48
  11.2 0.0 copy-done.3
  11.2 0.1 fusion.5
  11.3 23.0 %all-to-all-done = bf16[256,16,128]{2,0,1:T(8,128)(2,1)S(1)} async-done(((bf16[256,16,128]{2,0,1:T(8,128)(2,1)}), bf16[256,16,128]{2,0,1:T(8,128)(2,1)S(1)}, u32[]{:S(2)}, u32[]{:S(2)}) %all-to-all-start) | async-done | bytes 1048608 | tf_op jit(solution)/shard_map/all_to_all | solution.py:44
  34.3 0.0 copy-done
  34.3 0.0 copy-done.1
  34.3 5.1 %fusion = f32[1024,128]{1,0:T(8,128)S(1)} fusion(s32[4096]{0:T(1024)S(1)} %bitcast.23, bf16[4096,128]{1,0:T(8,128)(2,1)S(1)} %bitcast.22, pred[128]{0:T(512)(128)(4,1)S(1)} %iota_compare_fusion.3, bf16[1,128,128]{2,1,0:T(8,128)(2,1)S(1)} %copy-done), kind=kOutput, calls=%fused_computation.2 | convolution fusion | flops 1213202432 | bytes 1622144 | tf_op jit(solution)/shard_map/while/body/eval_jaxpr/dot_general | solution.py:30
  39.4 0.6 %gather_fusion = f32[32,128]{1,0:T(8,128)S(1)} fusion(f32[1024,128]{1,0:T(8,128)S(1)} %fusion, s32[1024]{0:T(1024)S(1)} %pad_clamp_fusion), kind=kCustom, calls=%fused_computation | custom fusion | bytes 32896 | tf_op jit(solution)/shard_map/jit(take_along_axis)/gather | solution.py:51
  40.0 0.1 bitcast_select_fusion
  40.1 2.4 %collective-permute-start = (f32[1,16,128]{2,1,0:T(8,128)S(1)}, f32[1,16,128]{2,1,0:T(8,128)S(1)}, u32[]{:S(2)}, u32[]{:S(2)}) collective-permute-start(f32[1,16,128]{2,1,0:T(8,128)S(1)} %constant_dynamic-slice_fusion), channel_id=1, source_target_pairs={{0,16},{16,0},{1,17},{17,1},{2,18},{18,2},{3,19},{19,3},{4,20},{20... | collective-permute-start | bytes 24584 | tf_op jit(solution)/shard_map/ppermute | solution.py:17
  42.5 1.0 %select_bitcast_fusion = f32[1,1,1024,128]{3,2,1,0:T(8,128)} fusion(f32[1024,128]{1,0:T(8,128)S(1)} %fusion, pred[1024]{0:T(1024)(128)(4,1)S(1)} %fusion.5), kind=kLoop, calls=%fused_computation.8 | loop fusion | flops 131072 | bytes 1049600 | tf_op jit(solution)/shard_map/broadcast_in_dim | solution.py:61
  43.5 0.0 collective-permute-done
  43.5 0.6 %dynamic-slice_add_fusion = f32[1,16,128]{2,1,0:T(8,128)} fusion(f32[1,16,128]{2,1,0:T(8,128)S(1)} %collective-permute-done, f32[1,32,128]{2,1,0:T(8,128)S(1)} %bitcast_select_fusion, s32[]{:T(128)S(6)} %select_n.61), kind=kLoop, calls=%fused_computation.13 | loop fusion | flops 2048 | bytes 24580 | tf_op jit(solution)/shard_map/add | solution.py:57
  (4 shorter events, 0.0 us)
Async XLA Ops:
  0.6 33.7 %copy-start = (bf16[1,128,128]{2,1,0:T(8,128)(2,1)S(1)}, bf16[1,128,128]{2,1,0:T(8,128)(2,1)}, u32[]{:S(2)}) copy-start(bf16[1,128,128]{2,1,0:T(8,128)(2,1)} %param.7) | copy-start | bytes 98308
  3.1 6.8 %copy-start.2 = (s32[16]{0:T(128)S(1)}, s32[16]{0:T(128)}, u32[]{:S(2)}) copy-start(s32[16]{0:T(128)} %param.8) | copy-start | bytes 196
  3.1 8.1 %copy-start.3 = (s32[1,32]{1,0:T(1,128)S(1)}, s32[1,32]{1,0:T(1,128)}, u32[]{:S(2)}) copy-start(s32[1,32]{1,0:T(1,128)} %param.9) | copy-start | bytes 388
  3.1 31.2 %copy-start.1 = (s32[1,4096]{1,0:T(1,128)S(1)}, s32[1,4096]{1,0:T(1,128)}, u32[]{:S(2)}) copy-start(s32[1,4096]{1,0:T(1,128)} %param.6) | copy-start | bytes 49156
  3.1 31.2 %all-to-all-start = ((bf16[256,16,128]{2,0,1:T(8,128)(2,1)}), bf16[256,16,128]{2,0,1:T(8,128)(2,1)S(1)}, u32[]{:S(2)}, u32[]{:S(2)}) async-start(bf16[256,16,128]{2,0,1:T(8,128)(2,1)} %copy.8), calls=%async_computation | async-start | bytes 2097152 | tf_op jit(solution)/shard_map/all_to_all | solution.py:44
  40.1 3.4 %collective-permute-start = (f32[1,16,128]{2,1,0:T(8,128)S(1)}, f32[1,16,128]{2,1,0:T(8,128)S(1)}, u32[]{:S(2)}, u32[]{:S(2)}) collective-permute-start(f32[1,16,128]{2,1,0:T(8,128)S(1)} %constant_dynamic-slice_fusion), channel_id=1, source_target_pairs={{0,16},{16,0},{1,17},{17,1},{2,18},{18,2},{3,19},{19,3},{4,20},{20... | collective-permute-start | bytes 24584 | tf_op jit(solution)/shard_map/ppermute | solution.py:17
where the time goes:
time: 44.4 us; the launch traced here: 44.1 us
  waiting for transfers between devices  23 us (52%)
  starting transfers between devices  9.21 us (21%)
  matrix products  5.13 us (12%)
  local copies, waits for them, and re-layouts  3.65 us (8%)
  other arithmetic  2.44 us (5%)
  between operations  0.69 us (2%)
    all_to_all x1, waiting for transfers between devices, shards(): lax.all_to_all(grad_out, 'tab', split_axis=1, concat_axis=0, tiled=True)  23 us
    all_to_all x1, starting transfers between devices, shards(): lax.all_to_all(grad_out, 'tab', split_axis=1, concat_axis=0, tiled=True)  6.8 us
    dot_general x1, matrix products, add_block(): lax.dot_general(onehot, piece_rows, (((0,), (0,)), ((), ())), preferred_e...  5.13 us
    unnamed x9, local copies, waits for them, and re-layouts  2.49 us
    ppermute x1, starting transfers between devices, swapped(): return lax.ppermute(block, axis, route)  2.41 us
    broadcast_in_dim x1, other arithmetic, shards(): return (cold_grad[None], hot_grad)  1 us
  transfers between devices with their start and end apart: 2, of which 1 were waited for; matrix products, arithmetic and copies ran while one was open for 5% of the time, Pallas kernels for 0%

commit v1 on v0

--- a/solution.py
+++ b/solution.py
@@ -41,7 +41,10 @@
     columns = lax.broadcasted_iota(jnp.int32, (1, 1, base_width), 2)
     first_table = lax.axis_index("tab") * tab_dev
     own_widths = lax.dynamic_slice_in_dim(widths, first_table, tab_dev, 0)
-    received = lax.all_to_all(grad_out, "tab", split_axis=1, concat_axis=0, tiled=True)
+    devices = lax.axis_size("tab")
+    parts = jnp.stack(jnp.split(grad_out, devices, axis=1), axis=0)
+    parts = lax.all_to_all(parts, "tab", split_axis=0, concat_axis=0)
+    received = jnp.concatenate(parts, axis=0)
     full_proj = jnp.einsum(
         "bte,tej->tbj", received, projections, preferred_element_type=jnp.float32
     )

time: 44.4 us -> 58.3 us (1.31)
  local copies, waits for them, and re-layouts: 3.65 us -> 17.6 us
    unnamed x9 -> x23, local copies, waits for them, and re-layouts: 2.49 us -> 9.46 us
    split x0 -> x1, local copies, waits for them, and re-layouts: none -> 6.32 us  [shards(): parts = jnp.stack(jnp.split(grad_out, devices, axis=1), axis=0)]
    another operation x0 -> x1, local copies, waits for them, and re-layouts: none -> 0.64 us  [shards(): parts = jnp.stack(jnp.split(grad_out, devices, axis=1), axis=0)]
  transfers between devices with their start and end apart: 2 -> 2, of which waited for: 1 -> 1; matrix products, arithmetic and copies ran while one was open for 5% -> 4% of each run, Pallas kernels for 0% -> 0%
where the time goes in v1:
time: 58.3 us; the launch traced here: 58.1 us
  waiting for transfers between devices  23 us (39%)
  local copies, waits for them, and re-layouts  17.6 us (30%)
  starting transfers between devices  9.21 us (16%)
  matrix products  5.13 us (9%)
  other arithmetic  2.44 us (4%)
  between operations  0.7 us (1%)
    all_to_all x1, waiting for transfers between devices, shards(): parts = lax.all_to_all(parts, 'tab', split_axis=0, concat_axis=0)  23 us
    unnamed x23, local copies, waits for them, and re-layouts  9.46 us
    all_to_all x1, starting transfers between devices, shards(): parts = lax.all_to_all(parts, 'tab', split_axis=0, concat_axis=0)  6.8 us
    split x1, local copies, waits for them, and re-layouts, shards(): parts = jnp.stack(jnp.split(grad_out, devices, axis=1), axis=0)  6.32 us
    dot_general x1, matrix products, add_block(): lax.dot_general(onehot, piece_rows, (((0,), (0,)), ((), ())), preferred_e...  5.13 us
    ppermute x1, starting transfers between devices, swapped(): return lax.ppermute(block, axis, route)  2.41 us
  transfers between devices with their start and end apart: 2, of which 1 were waited for; matrix products, arithmetic and copies ran while one was open for 4% of the time, Pallas kernels for 0%

profile of v1, /device:TPU:9, one launch (start us, length us, event | category | flops | bytes accessed | tf_op | source)
XLA Modules:
  0.0 58.1 jit_solution(6389287765299000777)
XLA Ops:
  0.6 0.0 copy-start
  0.6 6.3 %fusion.26 = (bf16[256,1,128]{2,1,0:T(2,128)(2,1)S(1)}, bf16[256,1,128]{2,1,0:T(2,128)(2,1)S(1)}, bf16[256,1,128]{2,1,0:T(2,128)(2,1)S(1)}, bf16[256,1,128]{2,1,...) fusion(bf16[256,16,128]{2,1,0:T(8,128)(2,1)} %param.5), kind=kLoop, calls=%fused_computation.54 | loop fusion | bytes 2097152 | tf_op jit(solution)/shard_map/split | solution.py:45
  7.0 0.6 %fusion.21 = bf16[16,256,1,128]{3,1,2,0:T(8,128)(2,1)} fusion(bf16[256,1,128]{2,1,0:T(2,128)(2,1)S(1)} %get-tuple-element.35), kind=kLoop, calls=%fused_computation.42 | loop fusion | bytes 131072
  7.6 0.6 %fusion.20 = bf16[16,256,1,128]{3,1,2,0:T(8,128)(2,1)} fusion(bf16[16,256,1,128]{3,1,2,0:T(8,128)(2,1)} %fusion.21, bf16[256,1,128]{2,1,0:T(2,128)(2,1)S(1)} %get-tuple-element.34), kind=kLoop, calls=%fused_computation.40 | loop fusion | bytes 131072
  8.2 0.6 %fusion.19 = bf16[16,256,1,128]{3,1,2,0:T(8,128)(2,1)} fusion(bf16[16,256,1,128]{3,1,2,0:T(8,128)(2,1)} %fusion.20, bf16[256,1,128]{2,1,0:T(2,128)(2,1)S(1)} %get-tuple-element.33), kind=kLoop, calls=%fused_computation.38 | loop fusion | bytes 131072
  8.9 0.6 %fusion.18 = bf16[16,256,1,128]{3,1,2,0:T(8,128)(2,1)} fusion(bf16[16,256,1,128]{3,1,2,0:T(8,128)(2,1)} %fusion.19, bf16[256,1,128]{2,1,0:T(2,128)(2,1)S(1)} %get-tuple-element.32), kind=kLoop, calls=%fused_computation.36 | loop fusion | bytes 131072
  9.5 0.6 %fusion.17 = bf16[16,256,1,128]{3,1,2,0:T(8,128)(2,1)} fusion(bf16[16,256,1,128]{3,1,2,0:T(8,128)(2,1)} %fusion.18, bf16[256,1,128]{2,1,0:T(2,128)(2,1)S(1)} %get-tuple-element.31), kind=kLoop, calls=%fused_computation.34 | loop fusion | bytes 131072
  10.1 0.6 %fusion.16 = bf16[16,256,1,128]{3,1,2,0:T(8,128)(2,1)} fusion(bf16[16,256,1,128]{3,1,2,0:T(8,128)(2,1)} %fusion.17, bf16[256,1,128]{2,1,0:T(2,128)(2,1)S(1)} %get-tuple-element.30), kind=kLoop, calls=%fused_computation.32 | loop fusion | bytes 131072
  10.8 0.6 %fusion.15 = bf16[16,256,1,128]{3,1,2,0:T(8,128)(2,1)} fusion(bf16[16,256,1,128]{3,1,2,0:T(8,128)(2,1)} %fusion.16, bf16[256,1,128]{2,1,0:T(2,128)(2,1)S(1)} %get-tuple-element.29), kind=kLoop, calls=%fused_computation.30 | loop fusion | bytes 131072
  11.4 0.6 %fusion.14 = bf16[16,256,1,128]{3,1,2,0:T(8,128)(2,1)} fusion(bf16[16,256,1,128]{3,1,2,0:T(8,128)(2,1)} %fusion.15, bf16[256,1,128]{2,1,0:T(2,128)(2,1)S(1)} %get-tuple-element.28), kind=kLoop, calls=%fused_computation.28 | loop fusion | bytes 131072
  12.0 0.6 %fusion.13 = bf16[16,256,1,128]{3,1,2,0:T(8,128)(2,1)} fusion(bf16[16,256,1,128]{3,1,2,0:T(8,128)(2,1)} %fusion.14, bf16[256,1,128]{2,1,0:T(2,128)(2,1)S(1)} %get-tuple-element.27), kind=kLoop, calls=%fused_computation.26 | loop fusion | bytes 131072
  12.6 0.6 %fusion.12 = bf16[16,256,1,128]{3,1,2,0:T(8,128)(2,1)} fusion(bf16[16,256,1,128]{3,1,2,0:T(8,128)(2,1)} %fusion.13, bf16[256,1,128]{2,1,0:T(2,128)(2,1)S(1)} %get-tuple-element.26), kind=kLoop, calls=%fused_computation.24 | loop fusion | bytes 131072
  13.3 0.6 %fusion.11 = bf16[16,256,1,128]{3,1,2,0:T(8,128)(2,1)} fusion(bf16[16,256,1,128]{3,1,2,0:T(8,128)(2,1)} %fusion.12, bf16[256,1,128]{2,1,0:T(2,128)(2,1)S(1)} %get-tuple-element.25), kind=kLoop, calls=%fused_computation.22 | loop fusion | bytes 131072
  13.9 0.6 %fusion.10 = bf16[16,256,1,128]{3,1,2,0:T(8,128)(2,1)} fusion(bf16[16,256,1,128]{3,1,2,0:T(8,128)(2,1)} %fusion.11, bf16[256,1,128]{2,1,0:T(2,128)(2,1)S(1)} %get-tuple-element.24), kind=kLoop, calls=%fused_computation.20 | loop fusion | bytes 131072
  14.5 0.6 %fusion.9 = bf16[16,256,1,128]{3,1,2,0:T(8,128)(2,1)} fusion(bf16[16,256,1,128]{3,1,2,0:T(8,128)(2,1)} %fusion.10, bf16[256,1,128]{2,1,0:T(2,128)(2,1)S(1)} %get-tuple-element.17), kind=kLoop, calls=%fused_computation.18 | loop fusion | bytes 131072
  15.2 0.6 %fusion.8 = bf16[16,256,1,128]{3,1,2,0:T(8,128)(2,1)} fusion(bf16[16,256,1,128]{3,1,2,0:T(8,128)(2,1)} %fusion.9, bf16[256,1,128]{2,1,0:T(2,128)(2,1)S(1)} %get-tuple-element.16), kind=kLoop, calls=%fused_computation.16 | loop fusion | bytes 131072
  15.8 0.6 %fusion.7 = bf16[16,256,1,128]{3,1,2,0:T(8,128)(2,1)} fusion(bf16[16,256,1,128]{3,1,2,0:T(8,128)(2,1)} %fusion.8, bf16[256,1,128]{2,1,0:T(2,128)(2,1)S(1)} %get-tuple-element.15), kind=kLoop, calls=%fused_computation.14 | loop fusion | bytes 131072
  16.4 0.6 %fusion.6 = bf16[16,256,1,128]{3,1,2,0:T(8,128)(2,1)} fusion(bf16[16,256,1,128]{3,1,2,0:T(8,128)(2,1)} %fusion.7, bf16[256,1,128]{2,1,0:T(2,128)(2,1)S(1)} %get-tuple-element.14), kind=kLoop, calls=%fused_computation.12 | loop fusion | bytes 131072 | tf_op jit(solution)/shard_map/stack | solution.py:45
  17.1 0.0 copy-start.2
  17.1 0.0 copy-start.3
  17.1 0.0 copy-start.1
  17.1 6.8 %all-to-all-start = ((bf16[16,256,1,128]{3,1,2,0:T(8,128)(2,1)}), bf16[16,256,1,128]{3,1,2,0:T(8,128)(2,1)S(1)}, u32[]{:S(2)}, u32[]{:S(2)}) async-start(bf16[16,256,1,128]{3,1,2,0:T(8,128)(2,1)} %fusion.6), calls=%async_computation | async-start | bytes 2097152 | tf_op jit(solution)/shard_map/all_to_all | solution.py:46
  23.9 0.0 copy-done.2
  23.9 0.6 %dynamic_slice.13 = s32[1]{0:T(128)} dynamic-slice(s32[16]{0:T(128)S(1)} %copy-done.2, s32[]{:T(128)S(6)} %select_n.55), dynamic_slice_sizes={1} | dynamic-slice | bytes 12 | tf_op jit(solution)/shard_map/dynamic_slice | solution.py:43
  24.5 0.6 %iota_compare_fusion.3 = pred[128]{0:T(512)(128)(4,1)S(1)} fusion(s32[]{:T(128)} %bitcast.2), kind=kLoop, calls=%fused_computation.52 | loop fusion | flops 128 | bytes 132 | tf_op jit(solution)/shard_map/lt | solution.py:51
  25.1 0.0 copy-done.3
  25.1 0.1 fusion.5
  25.3 23.0 %all-to-all-done = bf16[16,256,1,128]{3,1,2,0:T(8,128)(2,1)S(1)} async-done(((bf16[16,256,1,128]{3,1,2,0:T(8,128)(2,1)}), bf16[16,256,1,128]{3,1,2,0:T(8,128)(2,1)S(1)}, u32[]{:S(2)}, u32[]{:S(2)}) %all-to-all-start) | async-done | bytes 1048608 | tf_op jit(solution)/shard_map/all_to_all | solution.py:46
  48.2 0.0 copy-done
  48.2 0.0 copy-done.1
  48.2 5.1 %fusion = f32[1024,128]{1,0:T(8,128)S(1)} fusion(s32[4096]{0:T(1024)S(1)} %bitcast.83, bf16[4096,128]{1,0:T(8,128)(2,1)S(1)} %bitcast.82, pred[128]{0:T(512)(128)(4,1)S(1)} %iota_compare_fusion.3, bf16[1,128,128]{2,1,0:T(8,128)(2,1)S(1)} %copy-done), kind=kOutput, calls=%fused_computation.2 | convolution fusion | flops 1213202432 | bytes 1622144 | tf_op jit(solution)/shard_map/while/body/eval_jaxpr/dot_general | solution.py:30
  53.4 0.6 gather_fusion
  54.0 0.1 bitcast_select_fusion
  54.0 2.4 %collective-permute-start = (f32[1,16,128]{2,1,0:T(8,128)S(1)}, f32[1,16,128]{2,1,0:T(8,128)S(1)}, u32[]{:S(2)}, u32[]{:S(2)}) collective-permute-start(f32[1,16,128]{2,1,0:T(8,128)S(1)} %constant_dynamic-slice_fusion), channel_id=1, source_target_pairs={{0,16},{16,0},{1,17},{17,1},{2,18},{18,2},{3,19},{19,3},{4,20},{20... | collective-permute-start | bytes 24584 | tf_op jit(solution)/shard_map/ppermute | solution.py:17
  56.5 1.0 %select_bitcast_fusion = f32[1,1,1024,128]{3,2,1,0:T(8,128)} fusion(f32[1024,128]{1,0:T(8,128)S(1)} %fusion, pred[1024]{0:T(1024)(128)(4,1)S(1)} %fusion.5), kind=kLoop, calls=%fused_computation.8 | loop fusion | flops 131072 | bytes 1049600 | tf_op jit(solution)/shard_map/broadcast_in_dim | solution.py:64
  57.4 0.0 collective-permute-done
  57.5 0.6 %dynamic-slice_add_fusion = f32[1,16,128]{2,1,0:T(8,128)} fusion(f32[1,16,128]{2,1,0:T(8,128)S(1)} %collective-permute-done, f32[1,32,128]{2,1,0:T(8,128)S(1)} %bitcast_select_fusion, s32[]{:T(128)S(6)} %select_n.61), kind=kLoop, calls=%fused_computation.45 | loop fusion | flops 2048 | bytes 24580 | tf_op jit(solution)/shard_map/add | solution.py:60
  (4 shorter events, 0.0 us)
Async XLA Ops:
  0.6 47.6 %copy-start = (bf16[1,128,128]{2,1,0:T(8,128)(2,1)S(1)}, bf16[1,128,128]{2,1,0:T(8,128)(2,1)}, u32[]{:S(2)}) copy-start(bf16[1,128,128]{2,1,0:T(8,128)(2,1)} %param.7) | copy-start | bytes 98308
  17.1 6.8 %copy-start.2 = (s32[16]{0:T(128)S(1)}, s32[16]{0:T(128)}, u32[]{:S(2)}) copy-start(s32[16]{0:T(128)} %param.8) | copy-start | bytes 196
  17.1 8.1 %copy-start.3 = (s32[1,32]{1,0:T(1,128)S(1)}, s32[1,32]{1,0:T(1,128)}, u32[]{:S(2)}) copy-start(s32[1,32]{1,0:T(1,128)} %param.9) | copy-start | bytes 388
  17.1 31.2 %copy-start.1 = (s32[1,4096]{1,0:T(1,128)S(1)}, s32[1,4096]{1,0:T(1,128)}, u32[]{:S(2)}) copy-start(s32[1,4096]{1,0:T(1,128)} %param.6) | copy-start | bytes 49156
  17.1 31.2 %all-to-all-start = ((bf16[16,256,1,128]{3,1,2,0:T(8,128)(2,1)}), bf16[16,256,1,128]{3,1,2,0:T(8,128)(2,1)S(1)}, u32[]{:S(2)}, u32[]{:S(2)}) async-start(bf16[16,256,1,128]{3,1,2,0:T(8,128)(2,1)} %fusion.6), calls=%async_computation | async-start | bytes 2097152 | tf_op jit(solution)/shard_map/all_to_all | solution.py:46
  54.0 3.4 %collective-permute-start = (f32[1,16,128]{2,1,0:T(8,128)S(1)}, f32[1,16,128]{2,1,0:T(8,128)S(1)}, u32[]{:S(2)}, u32[]{:S(2)}) collective-permute-start(f32[1,16,128]{2,1,0:T(8,128)S(1)} %constant_dynamic-slice_fusion), channel_id=1, source_target_pairs={{0,16},{16,0},{1,17},{17,1},{2,18},{18,2},{3,19},{19,3},{4,20},{20... | collective-permute-start | bytes 24584 | tf_op jit(solution)/shard_map/ppermute | solution.py:17
